TPU v7x, 32 devices: a whole 2x2x4 slice. The times are simulated.
32 devices in a mesh: section: 2 (over x), expert: 16 (over z, y, core).
Axes of the slice: x: 2, y: 2, z: 4, core: 2. Of those that a mesh axis runs over, the one named last changes fastest.
Arguments:
- hidden_in: bfloat16 [2, 128, 3584], P(None, 'expert'), may hold values from -6 to 6
- layer_gain: float32 [2, 3584], P('section'), may hold values from 0.25 to 1.75
- router: bfloat16 [2, 3584, 4], P('section'), may hold values from -0.09375 to 0.09375
- w_gate: bfloat16 [2, 3584, 8192], P('section', None, 'expert'), may hold values from -0.09375 to 0.09375
- w_up: bfloat16 [2, 3584, 8192], P('section', None, 'expert'), may hold values from -0.09375 to 0.09375
- w_down: bfloat16 [2, 8192, 3584], P('section', 'expert'), may hold values from -0.125 to 0.125
- final_gain: float32 [3584], replicated, may hold values from 0.25 to 1.75
- head: bfloat16 [8192, 3584], P(('section', 'expert')), may hold values from -18.775102 to 18.775102
- routing: int32 [2, 2, 128, 2], P('section', None, 'expert'), may hold values from 0 to 3, all different within a row; in each aligned block of 8 rows (0 to 7, 8 to 15, ..., all dimensions but the last counted through in order) at most 4 rows name the same one
- targets: int32 [2, 128], replicated, may hold values from 0 to 8191
- seq_ids: int32 [2, 128], replicated, may hold values from 0 to 3, never falling along the last dimension, each value on 1 to 64 neighbouring positions
Outputs:
- token_logprob: float32 [2, 128], P(None, 'expert')
- seq_mean: float32 [2, 4], replicated
Inputs may be any that keep to these rules, and one draw needn't show every extreme that they name: `routing`: in each aligned block of 8 tokens (the tokens of one device) a token's 2 experts differ and no expert is named by more than 4 tokens; some expert is named by exactly 4. `seq_ids`: ids never fall along a micro-batch's tokens; each of the 4 ids occurs on 1 to 64 tokens, one on exactly 64.
All inputs are finite; a program needn't handle non-finite values.
Results may differ from a plain program's by a relative error of at most 0.014.
Values may be sent and summed in bfloat16 or wider, within the bound.
A program may use at most 64 MiB of HBM per device.

v0:
```python
import jax
import jax.numpy as jnp
from jax import lax
from jax.sharding import PartitionSpec as P

SEQS = 4


def shifted(shard, axis, by):
    size = lax.axis_size(axis)
    pairs = [(i, i + by) for i in range(size) if 0 <= i + by < size]
    return lax.ppermute(shard, axis, pairs)


def broadcast(block, axis, holder):
    block = jnp.where(lax.axis_index(axis) == holder, block, jnp.zeros_like(block))
    return lax.psum(block, axis)


def rms_scale(states, gain):
    values = states.astype(jnp.float32)
    factor = lax.rsqrt(jnp.mean(values * values, -1, keepdims=True) + 1e-06)
    return values * factor * gain


def body(
    hidden_in, layer_gain, router, w_gate, w_up, w_down, final_gain, head, routing, targets, seq_ids
):
    micro_count, tok_count, model_width = hidden_in.shape
    expert_count = router.shape[2]
    top_count = routing.shape[3]
    sections = lax.axis_size("section")
    members = lax.axis_size("expert")
    section_pos = lax.axis_index("section")
    member_pos = lax.axis_index("expert")
    split_count = members // expert_count
    capacity = min(tok_count, 9 * tok_count * top_count // (8 * expert_count))
    tick_count = micro_count + sections - 1

    def expert_rows(incoming):
        sources, slot_count, width_in = incoming.shape
        flat_rows = incoming.reshape(sources * slot_count, width_in)
        gate_val = jnp.dot(flat_rows, w_gate[0], preferred_element_type=jnp.float32)
        up_val = jnp.dot(flat_rows, w_up[0], preferred_element_type=jnp.float32)
        inner = (jax.nn.silu(gate_val) * up_val).astype(jnp.bfloat16)
        partial_value = jnp.dot(inner, w_down[0], preferred_element_type=jnp.float32).astype(
            jnp.bfloat16
        )
        return lax.all_to_all(
            partial_value.reshape(sources, slot_count, width_in),
            "expert",
            split_axis=0,
            concat_axis=0,
            tiled=True,
        )

    def expert_layer(states, micro_pos):
        route_ids = lax.dynamic_index_in_dim(routing[0], micro_pos, 0, keepdims=False)
        normed = rms_scale(states, layer_gain[0]).astype(jnp.bfloat16)
        logits = jnp.dot(normed, router[0], preferred_element_type=jnp.float32)
        chosen = route_ids[:, :, None] == jnp.arange(expert_count, dtype=jnp.int32)[None, None, :]
        affinity = jax.nn.sigmoid(jnp.sum(jnp.where(chosen, logits[:, None, :], 0.0), -1))
        weight = affinity / jnp.sum(affinity, -1, keepdims=True)
        flags = chosen.reshape(tok_count * top_count, expert_count).astype(jnp.int32)
        ranks = jnp.cumsum(flags, 0) - flags
        slot_ids = jnp.sum(ranks * flags, -1).reshape(tok_count, top_count)
        destination = route_ids * capacity + slot_ids
        places = jnp.arange(expert_count * capacity, dtype=jnp.int32)
        table = jnp.any(places[:, None, None] == destination[None], -1).astype(jnp.bfloat16)
        packed = jnp.dot(table, normed, preferred_element_type=jnp.float32).astype(jnp.bfloat16)
        outgoing = jnp.broadcast_to(
            packed.reshape(expert_count, 1, capacity, model_width),
            (expert_count, split_count, capacity, model_width),
        )
        outgoing = outgoing.reshape(members, capacity, model_width)
        returned = expert_rows(
            lax.all_to_all(outgoing, "expert", split_axis=0, concat_axis=0, tiled=True)
        )
        summed = jnp.sum(
            returned.reshape(expert_count, split_count, capacity, model_width).astype(jnp.float32),
            1,
        )
        summed = summed.reshape(expert_count * capacity, model_width)
        picked = summed[destination]
        mixed = jnp.sum(weight[:, :, None] * picked, 1)
        return (states.astype(jnp.float32) + 2.5 * mixed).astype(jnp.bfloat16)

    def advance(step, carry):
        arrived, record = carry
        entering = lax.dynamic_index_in_dim(
            hidden_in, jnp.minimum(step, micro_count - 1), 0, keepdims=False
        )
        states = jnp.where(section_pos == 0, entering, arrived)
        micro_pos = jnp.clip(step - section_pos, 0, micro_count - 1)
        result = expert_layer(states, micro_pos)
        finished = step - (sections - 1)
        record_pos = jnp.clip(finished, 0, micro_count - 1)
        keeping = (finished >= 0) & (section_pos == sections - 1)
        previous = lax.dynamic_index_in_dim(record, record_pos, 0, keepdims=False)
        record = lax.dynamic_update_index_in_dim(
            record, jnp.where(keeping, result, previous), record_pos, 0
        )
        arrived = shifted(result, "section", 1)
        return (arrived, record)

    start_rows = jnp.zeros((tok_count, model_width), jnp.bfloat16)
    start_record = jnp.zeros((micro_count, tok_count, model_width), jnp.bfloat16)
    arrived, record = lax.fori_loop(0, tick_count, advance, (start_rows, start_record))
    shared = broadcast(record, "section", sections - 1)
    normed = rms_scale(lax.all_gather(shared, "expert", axis=1, tiled=True), final_gain).astype(
        jnp.bfloat16
    )
    logits = jnp.einsum("mrd,vd->mrv", normed, head, preferred_element_type=jnp.float32)
    voc_count = head.shape[0]
    vocab_start = (section_pos * members + member_pos) * voc_count
    vocab_ids = vocab_start + jnp.arange(voc_count, dtype=jnp.int32)
    target_hit = targets[:, :, None] == vocab_ids[None, None, :]
    target_part = jnp.sum(jnp.where(target_hit, logits, 0.0), -1)
    local_max = jnp.max(logits, -1)
    peak = lax.pmax(local_max, ("section", "expert"))
    local_sum = jnp.sum(jnp.exp(logits - peak[..., None]), -1)
    total, target_logit = lax.psum((local_sum, target_part), ("section", "expert"))
    logprob = target_logit - (peak + jnp.log(total))
    token_part = lax.dynamic_slice_in_dim(logprob, member_pos * tok_count, tok_count, 1)
    member = seq_ids[:, :, None] == jnp.arange(SEQS, dtype=jnp.int32)[None, None, :]
    sums = jnp.sum(jnp.where(member, logprob[..., None], 0.0), 1)
    counts = jnp.sum(member.astype(jnp.float32), 1)
    return (token_part, sums / counts)


def solution(mesh):
    return jax.shard_map(
        body,
        mesh=mesh,
        in_specs=(
            P(None, "expert", None),
            P("section", None),
            P("section", None, None),
            P("section", None, "expert"),
            P("section", None, "expert"),
            P("section", "expert", None),
            P(),
            P(("section", "expert"), None),
            P("section", None, "expert", None),
            P(),
            P(),
        ),
        out_specs=(P(None, "expert"), P()),
        check_vma=False,
    )
```

profile of v0, /device:TPU:0, one launch (start us, length us, event | category | flops | bytes accessed | tf_op | source)
XLA Modules:
  0.0 332.3 jit_solution(14966221587501759313)
XLA Ops:
  7.3 167.9 %while.17 = (s32[]{:T(128)}, bf16[8,3584]{1,0:T(8,128)(2,1)S(1)}, bf16[2,8,3584]{2,1,0:T(8,128)(2,1)S(1)}, pred[]{:T(512)}, bf16[2,8,3584]{2,1,0:T(8,128)(2,1)},...) while((s32[]{:T(128)}, bf16[8,3584]{1,0:T(8,128)(2,1)S(1)}, ...), condition=%wide.region_9.10_spmd, body=%wide.region_0.9_spmd.sunk | while | flops 707251328 | bytes 21631636 | solution.py:108
  7.3 0.8 constant_dynamic-slice_fusion.6
  8.7 0.7 multiply_add_fusion.2
  9.5 1.0 fusion.70
  10.5 0.8 reduce.2
  11.5 0.9 broadcast_in_dim.134
  12.4 7.4 %all-to-all-start = ((bf16[16,4,3584]{2,1,0:T(4,128)(2,1)}), bf16[16,4,3584]{2,1,0:T(4,128)(2,1)S(1)}, u32[]{:S(2)}, u32[]{:S(2)}) async-start(bf16[16,4,3584]{2,1,0:T(4,128)(2,1)} %bitcast.77), calls=%async_computation | async-start | bytes 917504 | tf_op jit(solution)/shard_map/while/body/eval_jaxpr/all_to_all | solution.py:77
  20.0 0.7 compare_select_fusion.2
  20.8 0.7 fusion.73
  21.5 0.9 fusion.72
  22.5 10.5 %all-to-all-done = bf16[16,4,3584]{2,1,0:T(4,128)(2,1)S(1)} async-done(((bf16[16,4,3584]{2,1,0:T(4,128)(2,1)}), bf16[16,4,3584]{2,1,0:T(4,128)(2,1)S(1)}, u32[]{:S(2)}, u32[]{:S(2)}) %all-to-all-start) | async-done | bytes 458784 | tf_op jit(solution)/shard_map/while/body/eval_jaxpr/all_to_all | solution.py:77
  33.2 2.8 fusion.71
  35.9 4.6 %convolution_convert_fusion.5 = bf16[64,3584]{1,0:T(8,128)(2,1)S(1)} fusion(bf16[1,512,3584]{2,1,0:T(8,128)(2,1)} %get-tuple-element.450, bf16[64,3584]{1,0:T(8,128)(2,1)S(1)} %reshape.218, bf16[1,3584,512]{2,1,0:T(8,128)(2,1)} %get-tuple-element.449, f32[64,512]{1,0:T(8,128)S(1)} %fusion.71), kind=kOutput, calls=%fused_computation.1.clone.1 | convolution fusion | flops 470188032 | bytes 8388608 | tf_op jit(solution)/shard_map/while/body/eval_jaxpr/dot_general | solution.py:46
  40.6 0.9 reshape.219
  41.4 3.8 %all-to-all-start.1 = ((bf16[16,4,3584]{2,1,0:T(4,128)(2,1)}), bf16[16,4,3584]{2,1,0:T(4,128)(2,1)S(1)}, u32[]{:S(2)}, u32[]{:S(2)}) async-start(bf16[16,4,3584]{2,1,0:T(4,128)(2,1)} %reshape.219), calls=%async_computation.1 | async-start | bytes 917504 | tf_op jit(solution)/shard_map/while/body/eval_jaxpr/all_to_all | solution.py:49
  45.4 13.1 %all-to-all-done.1 = bf16[16,4,3584]{2,1,0:T(4,128)(2,1)S(1)} async-done(((bf16[16,4,3584]{2,1,0:T(4,128)(2,1)}), bf16[16,4,3584]{2,1,0:T(4,128)(2,1)S(1)}, u32[]{:S(2)}, u32[]{:S(2)}) %all-to-all-start.1) | async-done | bytes 458784 | tf_op jit(solution)/shard_map/while/body/eval_jaxpr/all_to_all | solution.py:49
  58.8 0.6 gather_fusion
  59.9 3.4 %collective-permute-start = (bf16[8,3584]{1,0:T(8,128)(2,1)S(1)}, bf16[8,3584]{1,0:T(8,128)(2,1)S(1)}, u32[]{:S(2)}, u32[]{:S(2)}) collective-permute-start(bf16[8,3584]{1,0:T(8,128)(2,1)S(1)} %get-tuple-element.401), channel_id=1, source_target_pairs={{0,16},{1,17},{2,18},{3,19},{4,20},{5,21},{6,22},{7,23},{8,24},{9,... | collective-permute-start | bytes 172040 | tf_op jit(solution)/shard_map/while/body/eval_jaxpr/ppermute | solution.py:12
  63.4 1.8 collective-permute-done
  65.2 0.7 constant_dynamic-slice_fusion.6
  66.5 0.7 multiply_add_fusion.2
  67.2 1.0 fusion.70
  68.2 0.8 reduce.2
  69.3 0.9 broadcast_in_dim.134
  70.1 3.8 %all-to-all-start = ((bf16[16,4,3584]{2,1,0:T(4,128)(2,1)}), bf16[16,4,3584]{2,1,0:T(4,128)(2,1)S(1)}, u32[]{:S(2)}, u32[]{:S(2)}) async-start(bf16[16,4,3584]{2,1,0:T(4,128)(2,1)} %bitcast.77), calls=%async_computation | async-start | bytes 917504 | tf_op jit(solution)/shard_map/while/body/eval_jaxpr/all_to_all | solution.py:77
  74.1 0.7 compare_select_fusion.2
  75.0 0.7 fusion.73
  75.6 0.9 fusion.72
  76.6 10.5 %all-to-all-done = bf16[16,4,3584]{2,1,0:T(4,128)(2,1)S(1)} async-done(((bf16[16,4,3584]{2,1,0:T(4,128)(2,1)}), bf16[16,4,3584]{2,1,0:T(4,128)(2,1)S(1)}, u32[]{:S(2)}, u32[]{:S(2)}) %all-to-all-start) | async-done | bytes 458784 | tf_op jit(solution)/shard_map/while/body/eval_jaxpr/all_to_all | solution.py:77
  87.3 2.8 fusion.71
  90.1 4.6 %convolution_convert_fusion.5 = bf16[64,3584]{1,0:T(8,128)(2,1)S(1)} fusion(bf16[1,512,3584]{2,1,0:T(8,128)(2,1)} %get-tuple-element.450, bf16[64,3584]{1,0:T(8,128)(2,1)S(1)} %reshape.218, bf16[1,3584,512]{2,1,0:T(8,128)(2,1)} %get-tuple-element.449, f32[64,512]{1,0:T(8,128)S(1)} %fusion.71), kind=kOutput, calls=%fused_computation.1.clone.1 | convolution fusion | flops 470188032 | bytes 8388608 | tf_op jit(solution)/shard_map/while/body/eval_jaxpr/dot_general | solution.py:46
  94.7 0.9 reshape.219
  95.6 3.8 %all-to-all-start.1 = ((bf16[16,4,3584]{2,1,0:T(4,128)(2,1)}), bf16[16,4,3584]{2,1,0:T(4,128)(2,1)S(1)}, u32[]{:S(2)}, u32[]{:S(2)}) async-start(bf16[16,4,3584]{2,1,0:T(4,128)(2,1)} %reshape.219), calls=%async_computation.1 | async-start | bytes 917504 | tf_op jit(solution)/shard_map/while/body/eval_jaxpr/all_to_all | solution.py:49
  99.5 13.1 %all-to-all-done.1 = bf16[16,4,3584]{2,1,0:T(4,128)(2,1)S(1)} async-done(((bf16[16,4,3584]{2,1,0:T(4,128)(2,1)}), bf16[16,4,3584]{2,1,0:T(4,128)(2,1)S(1)}, u32[]{:S(2)}, u32[]{:S(2)}) %all-to-all-start.1) | async-done | bytes 458784 | tf_op jit(solution)/shard_map/while/body/eval_jaxpr/all_to_all | solution.py:49
  112.9 0.6 gather_fusion
  114.1 4.3 %collective-permute-start = (bf16[8,3584]{1,0:T(8,128)(2,1)S(1)}, bf16[8,3584]{1,0:T(8,128)(2,1)S(1)}, u32[]{:S(2)}, u32[]{:S(2)}) collective-permute-start(bf16[8,3584]{1,0:T(8,128)(2,1)S(1)} %get-tuple-element.401), channel_id=1, source_target_pairs={{0,16},{1,17},{2,18},{3,19},{4,20},{5,21},{6,22},{7,23},{8,24},{9,... | collective-permute-start | bytes 172040 | tf_op jit(solution)/shard_map/while/body/eval_jaxpr/ppermute | solution.py:12
  118.4 1.8 collective-permute-done
  120.2 0.7 constant_dynamic-slice_fusion.6
  121.5 0.7 multiply_add_fusion.2
  122.3 1.0 fusion.70
  123.2 0.8 reduce.2
  124.3 0.9 broadcast_in_dim.134
  125.2 3.8 %all-to-all-start = ((bf16[16,4,3584]{2,1,0:T(4,128)(2,1)}), bf16[16,4,3584]{2,1,0:T(4,128)(2,1)S(1)}, u32[]{:S(2)}, u32[]{:S(2)}) async-start(bf16[16,4,3584]{2,1,0:T(4,128)(2,1)} %bitcast.77), calls=%async_computation | async-start | bytes 917504 | tf_op jit(solution)/shard_map/while/body/eval_jaxpr/all_to_all | solution.py:77
  129.1 0.7 compare_select_fusion.2
  130.0 0.7 fusion.73
  130.7 0.9 fusion.72
  131.7 10.5 %all-to-all-done = bf16[16,4,3584]{2,1,0:T(4,128)(2,1)S(1)} async-done(((bf16[16,4,3584]{2,1,0:T(4,128)(2,1)}), bf16[16,4,3584]{2,1,0:T(4,128)(2,1)S(1)}, u32[]{:S(2)}, u32[]{:S(2)}) %all-to-all-start) | async-done | bytes 458784 | tf_op jit(solution)/shard_map/while/body/eval_jaxpr/all_to_all | solution.py:77
  142.3 2.8 fusion.71
  145.1 4.6 %convolution_convert_fusion.5 = bf16[64,3584]{1,0:T(8,128)(2,1)S(1)} fusion(bf16[1,512,3584]{2,1,0:T(8,128)(2,1)} %get-tuple-element.450, bf16[64,3584]{1,0:T(8,128)(2,1)S(1)} %reshape.218, bf16[1,3584,512]{2,1,0:T(8,128)(2,1)} %get-tuple-element.449, f32[64,512]{1,0:T(8,128)S(1)} %fusion.71), kind=kOutput, calls=%fused_computation.1.clone.1 | convolution fusion | flops 470188032 | bytes 8388608 | tf_op jit(solution)/shard_map/while/body/eval_jaxpr/dot_general | solution.py:46
  149.7 0.9 reshape.219
  150.6 3.8 %all-to-all-start.1 = ((bf16[16,4,3584]{2,1,0:T(4,128)(2,1)}), bf16[16,4,3584]{2,1,0:T(4,128)(2,1)S(1)}, u32[]{:S(2)}, u32[]{:S(2)}) async-start(bf16[16,4,3584]{2,1,0:T(4,128)(2,1)} %reshape.219), calls=%async_computation.1 | async-start | bytes 917504 | tf_op jit(solution)/shard_map/while/body/eval_jaxpr/all_to_all | solution.py:49
  154.5 13.1 %all-to-all-done.1 = bf16[16,4,3584]{2,1,0:T(4,128)(2,1)S(1)} async-done(((bf16[16,4,3584]{2,1,0:T(4,128)(2,1)}), bf16[16,4,3584]{2,1,0:T(4,128)(2,1)S(1)}, u32[]{:S(2)}, u32[]{:S(2)}) %all-to-all-start.1) | async-done | bytes 458784 | tf_op jit(solution)/shard_map/while/body/eval_jaxpr/all_to_all | solution.py:49
  167.9 0.6 gather_fusion
  169.1 4.3 %collective-permute-start = (bf16[8,3584]{1,0:T(8,128)(2,1)S(1)}, bf16[8,3584]{1,0:T(8,128)(2,1)S(1)}, u32[]{:S(2)}, u32[]{:S(2)}) collective-permute-start(bf16[8,3584]{1,0:T(8,128)(2,1)S(1)} %get-tuple-element.401), channel_id=1, source_target_pairs={{0,16},{1,17},{2,18},{3,19},{4,20},{5,21},{6,22},{7,23},{8,24},{9,... | collective-permute-start | bytes 172040 | tf_op jit(solution)/shard_map/while/body/eval_jaxpr/ppermute | solution.py:12
  173.4 1.8 collective-permute-done
  175.2 0.6 broadcast_select_fusion
  175.9 21.4 %all-reduce.3.cloned.1.call-done = bf16[2,8,3584]{2,1,0:T(8,128)(2,1)} async-done(((bf16[2,8,3584]{2,1,0:T(8,128)(2,1)}), bf16[2,8,3584]{2,1,0:T(8,128)(2,1)}) %all-reduce.3.cloned.1.call-update) | async-done | bytes 114704 | tf_op jit(solution)/shard_map/psum | solution.py:17
  197.5 42.9 %all-gather.2.cloned.1.call-done = bf16[2,128,3584]{2,1,0:T(8,128)(2,1)} async-done(((bf16[2,8,3584]{2,1,0:T(8,128)(2,1)}), bf16[2,128,3584]{2,1,0:T(8,128)(2,1)}) %all-gather.2.cloned.1.call-update) | async-done | bytes 1835024 | tf_op jit(solution)/shard_map/all_gather | solution.py:110
  240.4 1.9 fusion.30
  242.4 2.3 fusion.39
  244.6 38.4 %pmax.7 = f32[2,128]{1,0:T(2,128)S(1)} all-reduce(f32[2,128]{1,0:T(2,128)S(1)} %get-tuple-element.314), channel_id=1, replica_groups=mesh['section'=2,'expert'=16] {'section','expert'}, use_global_device_ids=true, to_apply=%region_15.16 | all-reduce | flops 256 | bytes 2048 | tf_op jit(solution)/shard_map/pmax | solution.py:120
  283.3 40.9 %all-reduce = (f32[2,128]{1,0:T(2,128)S(1)}, f32[2,128]{1,0:T(2,128)S(1)}) all-reduce(f32[2,128]{1,0:T(2,128)S(1)} %get-tuple-element.279, f32[2,128]{1,0:T(2,128)S(1)} %get-tuple-element.278), channel_id=1, replica_groups=mesh['section'=2,'expert'=16] {'section','expert'}, use_global_device_ids=true, to_apply=%region_13.14 | all-reduce | flops 512 | bytes 4096 | tf_op jit(solution)/shard_map/psum | solution.py:122
  324.3 0.6 constant_dynamic-slice_fusion.2
  324.9 0.6 div.62
  (100 shorter events, 7.7 us)
Async XLA Ops:
  7.2 235.2 %copy-start = (bf16[256,3584]{1,0:T(8,128)(2,1)S(1)}, bf16[256,3584]{1,0:T(8,128)(2,1)}, u32[]{:S(2)}) copy-start(bf16[256,3584]{1,0:T(8,128)(2,1)} %param.20) | copy-start | bytes 5505028
  7.2 190.2 %all-reduce.3.cloned.1.call-start = ((), (), s32[]{:S(2)}) async-start(), calls=%async_computation.2 | async-start | bytes 229376 | tf_op jit(solution)/shard_map/psum | solution.py:17
  7.3 235.1 %copy-start.3 = (f32[3584]{0:T(1024)S(1)}, f32[3584]{0:T(1024)}, u32[]{:S(2)}) copy-start(f32[3584]{0:T(1024)} %param.19) | copy-start | bytes 43012
  12.4 20.6 %all-to-all-start = ((bf16[16,4,3584]{2,1,0:T(4,128)(2,1)}), bf16[16,4,3584]{2,1,0:T(4,128)(2,1)S(1)}, u32[]{:S(2)}, u32[]{:S(2)}) async-start(bf16[16,4,3584]{2,1,0:T(4,128)(2,1)} %bitcast.77), calls=%async_computation | async-start | bytes 917504 | tf_op jit(solution)/shard_map/while/body/eval_jaxpr/all_to_all | solution.py:77
  41.4 17.0 %all-to-all-start.1 = ((bf16[16,4,3584]{2,1,0:T(4,128)(2,1)}), bf16[16,4,3584]{2,1,0:T(4,128)(2,1)S(1)}, u32[]{:S(2)}, u32[]{:S(2)}) async-start(bf16[16,4,3584]{2,1,0:T(4,128)(2,1)} %reshape.219), calls=%async_computation.1 | async-start | bytes 917504 | tf_op jit(solution)/shard_map/while/body/eval_jaxpr/all_to_all | solution.py:49
  59.9 5.2 %collective-permute-start = (bf16[8,3584]{1,0:T(8,128)(2,1)S(1)}, bf16[8,3584]{1,0:T(8,128)(2,1)S(1)}, u32[]{:S(2)}, u32[]{:S(2)}) collective-permute-start(bf16[8,3584]{1,0:T(8,128)(2,1)S(1)} %get-tuple-element.401), channel_id=1, source_target_pairs={{0,16},{1,17},{2,18},{3,19},{4,20},{5,21},{6,22},{7,23},{8,24},{9,... | collective-permute-start | bytes 172040 | tf_op jit(solution)/shard_map/while/body/eval_jaxpr/ppermute | solution.py:12
  70.1 17.0 %all-to-all-start = ((bf16[16,4,3584]{2,1,0:T(4,128)(2,1)}), bf16[16,4,3584]{2,1,0:T(4,128)(2,1)S(1)}, u32[]{:S(2)}, u32[]{:S(2)}) async-start(bf16[16,4,3584]{2,1,0:T(4,128)(2,1)} %bitcast.77), calls=%async_computation | async-start | bytes 917504 | tf_op jit(solution)/shard_map/while/body/eval_jaxpr/all_to_all | solution.py:77
  95.6 17.0 %all-to-all-start.1 = ((bf16[16,4,3584]{2,1,0:T(4,128)(2,1)}), bf16[16,4,3584]{2,1,0:T(4,128)(2,1)S(1)}, u32[]{:S(2)}, u32[]{:S(2)}) async-start(bf16[16,4,3584]{2,1,0:T(4,128)(2,1)} %reshape.219), calls=%async_computation.1 | async-start | bytes 917504 | tf_op jit(solution)/shard_map/while/body/eval_jaxpr/all_to_all | solution.py:49
  114.1 6.1 %collective-permute-start = (bf16[8,3584]{1,0:T(8,128)(2,1)S(1)}, bf16[8,3584]{1,0:T(8,128)(2,1)S(1)}, u32[]{:S(2)}, u32[]{:S(2)}) collective-permute-start(bf16[8,3584]{1,0:T(8,128)(2,1)S(1)} %get-tuple-element.401), channel_id=1, source_target_pairs={{0,16},{1,17},{2,18},{3,19},{4,20},{5,21},{6,22},{7,23},{8,24},{9,... | collective-permute-start | bytes 172040 | tf_op jit(solution)/shard_map/while/body/eval_jaxpr/ppermute | solution.py:12
  125.2 17.0 %all-to-all-start = ((bf16[16,4,3584]{2,1,0:T(4,128)(2,1)}), bf16[16,4,3584]{2,1,0:T(4,128)(2,1)S(1)}, u32[]{:S(2)}, u32[]{:S(2)}) async-start(bf16[16,4,3584]{2,1,0:T(4,128)(2,1)} %bitcast.77), calls=%async_computation | async-start | bytes 917504 | tf_op jit(solution)/shard_map/while/body/eval_jaxpr/all_to_all | solution.py:77
  150.6 17.0 %all-to-all-start.1 = ((bf16[16,4,3584]{2,1,0:T(4,128)(2,1)}), bf16[16,4,3584]{2,1,0:T(4,128)(2,1)S(1)}, u32[]{:S(2)}, u32[]{:S(2)}) async-start(bf16[16,4,3584]{2,1,0:T(4,128)(2,1)} %reshape.219), calls=%async_computation.1 | async-start | bytes 917504 | tf_op jit(solution)/shard_map/while/body/eval_jaxpr/all_to_all | solution.py:49
  169.1 6.1 %collective-permute-start = (bf16[8,3584]{1,0:T(8,128)(2,1)S(1)}, bf16[8,3584]{1,0:T(8,128)(2,1)S(1)}, u32[]{:S(2)}, u32[]{:S(2)}) collective-permute-start(bf16[8,3584]{1,0:T(8,128)(2,1)S(1)} %get-tuple-element.401), channel_id=1, source_target_pairs={{0,16},{1,17},{2,18},{3,19},{4,20},{5,21},{6,22},{7,23},{8,24},{9,... | collective-permute-start | bytes 172040 | tf_op jit(solution)/shard_map/while/body/eval_jaxpr/ppermute | solution.py:12
  175.9 64.5 %all-gather.2.cloned.1.call-start = ((), (), s32[]{:S(2)}) async-start(), calls=%async_computation.3 | async-start | bytes 1949696 | tf_op jit(solution)/shard_map/all_gather | solution.py:110
  197.4 85.6 %copy-start.1 = (s32[2,128]{1,0:T(2,128)S(1)}, s32[2,128]{1,0:T(2,128)}, u32[]{:S(2)}) copy-start(s32[2,128]{1,0:T(2,128)} %param.22) | copy-start | bytes 3076
  197.4 126.7 %copy-start.2 = (s32[2,128]{1,0:T(2,128)S(1)}, s32[2,128]{1,0:T(2,128)}, u32[]{:S(2)}) copy-start(s32[2,128]{1,0:T(2,128)} %param.23) | copy-start | bytes 3076
Sparse Core Ops, SparseCore 0:
  176.0 21.3 all-reduce.2
  199.7 40.6 all-gather.1
where the time goes:
time: 334 us; the launch traced here: 332 us
  waiting for transfers between devices  141 us (42%)
  blocking collectives  79.3 us (24%)
  starting transfers between devices  38.5 us (12%)
  matrix products  28 us (8%)
  other arithmetic  16 us (5%)
  local copies, waits for them, and re-layouts  15.4 us (5%)
  between operations  14.1 us (4%)
    all_gather x1, waiting for transfers between devices, body(): lax.all_gather(shared, 'expert', axis=1, tiled=True)  42.9 us
    psum x1, blocking collectives, body(): lax.psum((local_sum, target_part), ('section', 'expert'))  40.9 us
    all_to_all x3, waiting for transfers between devices, expert_rows(): lax.all_to_all(partial_value.reshape(sources, slot_count, width_in), 'exp...  39.2 us
    pmax x1, blocking collectives, body(): peak = lax.pmax(local_max, ('section', 'expert'))  38.4 us
    all_to_all x3, waiting for transfers between devices, expert_layer(): lax.all_to_all(outgoing, 'expert', split_axis=0, concat_axis=0, tiled=True)  31.6 us
    psum x1, waiting for transfers between devices, broadcast(): return lax.psum(block, axis)  21.4 us
    all_to_all x3, starting transfers between devices, expert_layer(): lax.all_to_all(outgoing, 'expert', split_axis=0, concat_axis=0, tiled=True)  15 us
    dot_general x3, matrix products, expert_rows(): jnp.dot(inner, w_down[0], preferred_element_type=jnp.float32)  13.8 us
  transfers between devices with their start and end apart: 11, of which 11 were waited for; matrix products, arithmetic and copies ran while one was open for 3% of the time, Pallas kernels for 0%

commit v1 on v0

v1 whole, which is shorter than its diff:
```python
import functools

import jax
import jax.numpy as jnp
from jax import lax
from jax.experimental import pallas as pl
from jax.experimental.pallas import tpu as pltpu
from jax.sharding import PartitionSpec as P

SEQS = 4
CHUNKS = 2
F32 = jnp.float32
BF16 = jnp.bfloat16


def rms_scale(states, gain):
    values = states.astype(F32)
    factor = lax.rsqrt(jnp.mean(values * values, -1, keepdims=True) + 1e-06)
    return values * factor * gain


def kernel(
    dims,
    hid, gain, router, wg_hbm, wu_hbm, wd_hbm, fgain, head_hbm, route, tgt, seq,
    tok_out, seq_out,
    wg, wu, wd, head, stin, stout, pack, xbuf, pf, pb, cr, qf, qb, yr, sb, ret, fin, nb, stats,
    loc, dz, dy, dc, rc, ry, rz, xs, xr, fs, fr, az, ay, ac, ss, sr,
):
    S, E, J, C, R, M, T, cap, K = dims
    F = J * C
    members = E * F
    N = S * members
    MT = M * T
    D = stin.shape[1]
    Dc = D // K
    NT = members * MT
    sec = lax.axis_index("section")
    mem = lax.axis_index("expert")
    e = mem // F
    j = (mem % F) // C
    c = mem % C
    me = sec * members + mem
    voc = head.shape[0]
    cols = [pl.ds(k * Dc, Dc) for k in range(K)]

    def member(pe, pj, pc):
        return pe * F + pj * C + pc

    def remote(src, dst, send, recv, section, target):
        return pltpu.make_async_remote_copy(
            src_ref=src, dst_ref=dst, send_sem=send, recv_sem=recv,
            device_id=(section, target), device_id_type=pl.DeviceIdType.MESH,
        )

    locals_ = [
        pltpu.make_async_copy(wg_hbm, wg, loc.at[0]),
        pltpu.make_async_copy(wu_hbm, wu, loc.at[1]),
        pltpu.make_async_copy(wd_hbm, wd, loc.at[2]),
        pltpu.make_async_copy(head_hbm, head, loc.at[3]),
    ]
    load_hid = pltpu.make_async_copy(hid, stin, loc.at[4])

    @pl.when(sec == 0)
    def _():
        load_hid.start()

    for copy in locals_:
        copy.start()

    barrier = pltpu.get_barrier_semaphore()

    def greet(d, carry):
        peer = (me + d) % N
        pl.semaphore_signal(
            barrier, inc=1, device_id=(peer // members, peer % members),
            device_id_type=pl.DeviceIdType.MESH,
        )
        return carry

    lax.fori_loop(1, N, greet, 0)

    lanes = lax.broadcasted_iota(jnp.int32, (MT, E * R), 1)
    rows = lax.broadcasted_iota(jnp.int32, (MT, E * R), 0)
    hit = route[:, 0:1] == lanes // R
    for k in range(1, route.shape[1]):
        hit = hit | (route[:, k : k + 1] == lanes // R)
    hit_f = hit.astype(F32)
    row_a = lax.broadcasted_iota(jnp.int32, (MT, MT), 0)
    row_b = lax.broadcasted_iota(jnp.int32, (MT, MT), 1)
    earlier = ((row_b < row_a) & (row_a // T == row_b // T)).astype(BF16)
    rank = jnp.dot(earlier, hit_f.astype(BF16), preferred_element_type=F32)
    place = rank + ((rows // T) * cap).astype(F32)
    table = jnp.where(hit & (place == (lanes % R).astype(F32)), 1.0, 0.0).astype(F32)

    pl.semaphore_wait(barrier, N - 1)

    sends = []

    @pl.when(sec == 0)
    def _():
        load_hid.wait()

    @pl.when(sec > 0)
    def _():
        for k in range(K):
            remote(stout.at[:, cols[k]], stin.at[:, cols[k]], xs.at[k], xr.at[k], sec, mem).wait_recv()

    states = stin[...]
    normed = rms_scale(states, gain[...]).astype(BF16)

    table_b = table.astype(BF16)
    for k in range(K):
        packed = lax.dot_general(
            table_b, normed[:, k * Dc : (k + 1) * Dc], (((0,), (0,)), ((), ())),
            preferred_element_type=F32,
        ).reshape(E, R, Dc)
        pack[:, :, cols[k]] = packed.astype(BF16)
        for d in range(1, E):
            pe = (e + d) % E
            copy = remote(
                pack.at[pe, :, cols[k]], xbuf.at[c, j, e, :, cols[k]],
                dz.at[0, k, d], dz.at[1, k, d], sec, member(pe, j, c),
            )
            copy.start()
            sends.append(copy)
        xbuf[c, j, e, :, cols[k]] = pack[e, :, cols[k]]

    logits = lax.dot_general(
        normed, router[...], (((1,), (1,)), ((), ())), preferred_element_type=F32
    )
    spread = jnp.zeros((MT, E * R), F32)
    for i in range(E):
        spread = jnp.where(lanes // R == i, logits[:, i : i + 1], spread)
    weight = jax.nn.sigmoid(spread) * table
    weight = weight / jnp.sum(weight, -1, keepdims=True)
    weight_hi = weight.astype(BF16)
    weight_lo = (weight - weight_hi.astype(F32)).astype(BF16)

    for k in range(K):
        for d in range(1, E):
            se = (e + E - d) % E
            remote(
                pack.at[se, :, cols[k]], xbuf.at[c, j, se, :, cols[k]],
                dz.at[0, k, d], dz.at[1, k, d], sec, member(se, j, c),
            ).wait_recv()
        for d in range(1, J):
            copy = remote(
                xbuf.at[c, j, :, :, cols[k]], xbuf.at[c, j, :, :, cols[k]],
                dy.at[0, k, d], dy.at[1, k, d], sec, member(e, (j + d) % J, c),
            )
            copy.start()
            sends.append(copy)
    for k in range(K):
        for d in range(1, J):
            sj = (j + J - d) % J
            remote(
                xbuf.at[c, sj, :, :, cols[k]], xbuf.at[c, sj, :, :, cols[k]],
                dy.at[0, k, d], dy.at[1, k, d], sec, member(e, sj, c),
            ).wait_recv()
        for d in range(1, C):
            copy = remote(
                xbuf.at[c, :, :, :, cols[k]], xbuf.at[c, :, :, :, cols[k]],
                dc.at[0, k, d], dc.at[1, k, d], sec, member(e, j, (c + d) % C),
            )
            copy.start()
            sends.append(copy)

    locals_[0].wait()
    locals_[1].wait()
    gate_val = up_val = None
    for k in range(K):
        for d in range(1, C):
            sc = (c + C - d) % C
            remote(
                xbuf.at[sc, :, :, :, cols[k]], xbuf.at[sc, :, :, :, cols[k]],
                dc.at[0, k, d], dc.at[1, k, d], sec, member(e, j, sc),
            ).wait_recv()
        flat = xbuf[:, :, :, :, cols[k]].astype(F32).reshape(C * J * E * R, Dc).astype(BF16)
        g = jnp.dot(flat, wg[cols[k], :], preferred_element_type=F32)
        u = jnp.dot(flat, wu[cols[k], :], preferred_element_type=F32)
        gate_val = g if gate_val is None else gate_val + g
        up_val = u if up_val is None else up_val + u
    inner = (jax.nn.silu(gate_val) * up_val).astype(BF16)

    locals_[2].wait()
    for k in range(K):
        part = jnp.dot(inner, wd[:, cols[k]], preferred_element_type=F32)
        pf[:, :, :, :, cols[k]] = part.reshape(C, J, E, R, Dc)
        for d in range(1, C):
            pc = (c + d) % C
            pb[d, :, :, :, cols[k]] = pf[pc, :, :, :, cols[k]].astype(BF16)
            copy = remote(
                pb.at[d, :, :, :, cols[k]], cr.at[d, :, :, :, cols[k]],
                rc.at[0, k, d], rc.at[1, k, d], sec, member(e, j, pc),
            )
            copy.start()
            sends.append(copy)
    for k in range(K):
        total = pf[c, :, :, :, cols[k]]
        for d in range(1, C):
            remote(
                pb.at[d, :, :, :, cols[k]], cr.at[d, :, :, :, cols[k]],
                rc.at[0, k, d], rc.at[1, k, d], sec, member(e, j, (c + C - d) % C),
            ).wait_recv()
            total = total + cr[d, :, :, :, cols[k]].astype(F32)
        qf[:, :, :, cols[k]] = total
        for d in range(1, J):
            pj = (j + d) % J
            qb[d, :, :, cols[k]] = qf[pj, :, :, cols[k]].astype(BF16)
            copy = remote(
                qb.at[d, :, :, cols[k]], yr.at[d, :, :, cols[k]],
                ry.at[0, k, d], ry.at[1, k, d], sec, member(e, pj, c),
            )
            copy.start()
            sends.append(copy)
    for k in range(K):
        total = qf[j, :, :, cols[k]]
        for d in range(1, J):
            remote(
                qb.at[d, :, :, cols[k]], yr.at[d, :, :, cols[k]],
                ry.at[0, k, d], ry.at[1, k, d], sec, member(e, (j + J - d) % J, c),
            ).wait_recv()
            total = total + yr[d, :, :, cols[k]].astype(F32)
        sb[:, :, cols[k]] = total.astype(BF16)
        for d in range(1, E):
            pe = (e + d) % E
            copy = remote(
                sb.at[pe, :, cols[k]], ret.at[e, :, cols[k]],
                rz.at[0, k, d], rz.at[1, k, d], sec, member(pe, j, c),
            )
            copy.start()
            sends.append(copy)
        ret[e, :, cols[k]] = sb[e, :, cols[k]]

    def hand_on(k):
        return remote(stout.at[:, cols[k]], stin.at[:, cols[k]], xs.at[k], xr.at[k], sec + 1, mem)

    def spread_out(k, d):
        return remote(
            fin.at[c, j, e, :, cols[k]], fin.at[c, j, e, :, cols[k]],
            fs.at[k, d], fr.at[k], sec - d, mem,
        )

    for k in range(K):
        for d in range(1, E):
            se = (e + E - d) % E
            remote(
                sb.at[se, :, cols[k]], ret.at[se, :, cols[k]],
                rz.at[0, k, d], rz.at[1, k, d], sec, member(se, j, c),
            ).wait_recv()
        back = ret[:, :, cols[k]].astype(F32).reshape(E * R, Dc).astype(BF16)
        mixed = jnp.dot(weight_hi, back, preferred_element_type=F32) + jnp.dot(
            weight_lo, back, preferred_element_type=F32
        )
        result = (states[:, k * Dc : (k + 1) * Dc].astype(F32) + 2.5 * mixed).astype(BF16)

        @pl.when(sec < S - 1)
        def _():
            stout[:, cols[k]] = result
            hand_on(k).start()

        @pl.when(sec == S - 1)
        def _():
            fin[c, j, e, :, cols[k]] = result
            for d in range(1, S):
                spread_out(k, d).start()

    for k in range(K):
        @pl.when(sec < S - 1)
        def _():
            spread_out(k, 0).wait_recv()

        for d in range(1, E):
            copy = remote(
                fin.at[c, j, e, :, cols[k]], fin.at[c, j, e, :, cols[k]],
                az.at[0, k, d], az.at[1, k, d], sec, member((e + d) % E, j, c),
            )
            copy.start()
            sends.append(copy)
    for k in range(K):
        for d in range(1, E):
            se = (e + E - d) % E
            remote(
                fin.at[c, j, se, :, cols[k]], fin.at[c, j, se, :, cols[k]],
                az.at[0, k, d], az.at[1, k, d], sec, member(se, j, c),
            ).wait_recv()
        for d in range(1, J):
            copy = remote(
                fin.at[c, j, :, :, cols[k]], fin.at[c, j, :, :, cols[k]],
                ay.at[0, k, d], ay.at[1, k, d], sec, member(e, (j + d) % J, c),
            )
            copy.start()
            sends.append(copy)
    for k in range(K):
        for d in range(1, J):
            sj = (j + J - d) % J
            remote(
                fin.at[c, sj, :, :, cols[k]], fin.at[c, sj, :, :, cols[k]],
                ay.at[0, k, d], ay.at[1, k, d], sec, member(e, sj, c),
            ).wait_recv()
        for d in range(1, C):
            copy = remote(
                fin.at[c, :, :, :, cols[k]], fin.at[c, :, :, :, cols[k]],
                ac.at[0, k, d], ac.at[1, k, d], sec, member(e, j, (c + d) % C),
            )
            copy.start()
            sends.append(copy)
    for k in range(K):
        for d in range(1, C):
            sc = (c + C - d) % C
            remote(
                fin.at[sc, :, :, :, cols[k]], fin.at[sc, :, :, :, cols[k]],
                ac.at[0, k, d], ac.at[1, k, d], sec, member(e, j, sc),
            ).wait_recv()

    for pc in range(C):
        for pj in range(J):
            block = fin[pc, pj].reshape(E * MT, D)
            base = (pc * J + pj) * E * MT
            nb[base : base + E * MT, :] = rms_scale(block, fgain[...]).astype(BF16)
    locals_[3].wait()
    scores = lax.dot_general(
        head[...], nb[...], (((1,), (1,)), ((), ())), preferred_element_type=F32
    )
    vocab = me * voc + lax.broadcasted_iota(jnp.int32, (voc, NT), 0)
    own_target = jnp.sum(jnp.where(vocab == tgt[...], scores, 0.0), 0, keepdims=True)
    own_max = jnp.max(scores, 0, keepdims=True)
    own_sum = jnp.sum(jnp.exp(scores - own_max), 0, keepdims=True)
    stats[me, :, 0:NT] = own_max
    stats[me, :, NT : 2 * NT] = own_sum
    stats[me, :, 2 * NT : 3 * NT] = own_target

    def tell(d):
        peer = (me + d) % N
        return remote(
            stats.at[me], stats.at[me], ss.at[d], sr.at[d], peer // members, peer % members
        )

    def hear(d):
        peer = (me + N - d) % N
        return remote(
            stats.at[peer], stats.at[peer], ss.at[d], sr.at[d], peer // members, peer % members
        )

    def tell_all(d, carry):
        tell(d).start()
        return carry

    def hear_all(d, carry):
        hear(d).wait_recv()
        return carry

    lax.fori_loop(1, N, tell_all, 0)
    lax.fori_loop(1, N, hear_all, 0)
    maxes = stats[:, :, 0:NT]
    peak = jnp.max(maxes, 0)
    total = jnp.sum(jnp.exp(maxes - peak[None]) * stats[:, :, NT : 2 * NT], 0)
    target_logit = jnp.sum(stats[:, :, 2 * NT : 3 * NT], 0)
    logprob = target_logit - (peak + jnp.log(total))

    own = ((c * J + j) * E + e) * MT
    lane = lax.broadcasted_iota(jnp.int32, (MT, NT), 1)
    row = lax.broadcasted_iota(jnp.int32, (MT, NT), 0)
    tok_out[...] = jnp.sum(jnp.where(lane == own + row, logprob, 0.0), -1, keepdims=True)
    lane = lax.broadcasted_iota(jnp.int32, (M * SEQS, NT), 1)
    row = lax.broadcasted_iota(jnp.int32, (M * SEQS, NT), 0)
    inside = ((lane % MT) // T == row // SEQS) & (seq[...] == row % SEQS)
    sums = jnp.sum(jnp.where(inside, logprob, 0.0), -1, keepdims=True)
    counts = jnp.sum(jnp.where(inside, 1.0, 0.0), -1, keepdims=True)
    seq_out[...] = sums / counts

    for copy in sends:
        copy.wait_send()

    @pl.when(sec < S - 1)
    def _():
        for k in range(K):
            hand_on(k).wait_send()

    @pl.when(sec == S - 1)
    def _():
        for k in range(K):
            for d in range(1, S):
                spread_out(k, d).wait_send()

    def told_all(d, carry):
        tell(d).wait_send()
        return carry

    lax.fori_loop(1, N, told_all, 0)


def body(
    hidden_in, layer_gain, router, w_gate, w_up, w_down, final_gain, head, routing, targets, seq_ids
):
    M, T, D = hidden_in.shape
    E = router.shape[2]
    top = routing.shape[3]
    S = lax.axis_size("section")
    members = lax.axis_size("expert")
    F = members // E
    C = 2 if F % 2 == 0 else 1
    J = F // C
    cap = min(T, 9 * T * top // (8 * E))
    R = -(-M * cap // 8) * 8
    K = CHUNKS
    MT = M * T
    NT = members * MT
    ff = w_gate.shape[2]
    voc = head.shape[0]
    N = S * members
    dims = (S, E, J, C, R, M, T, cap, K)

    both = jnp.stack([targets, seq_ids]).reshape(2, M, E, J, C, T)
    both = both.transpose(0, 4, 3, 2, 1, 5).reshape(2, NT)

    vmem = pl.BlockSpec(memory_space=pltpu.VMEM)
    hbm = pl.BlockSpec(memory_space=pl.ANY)
    dma = pltpu.SemaphoreType.DMA
    tok, seq = pl.pallas_call(
        functools.partial(kernel, dims),
        out_shape=(
            jax.ShapeDtypeStruct((MT, 1), F32),
            jax.ShapeDtypeStruct((M * SEQS, 1), F32),
        ),
        in_specs=[hbm, vmem, vmem, hbm, hbm, hbm, vmem, hbm, vmem, vmem, vmem],
        out_specs=(vmem, vmem),
        scratch_shapes=[
            pltpu.VMEM((D, ff), BF16),
            pltpu.VMEM((D, ff), BF16),
            pltpu.VMEM((ff, D), BF16),
            pltpu.VMEM((voc, D), BF16),
            pltpu.VMEM((MT, D), BF16),
            pltpu.VMEM((MT, D), BF16),
            pltpu.VMEM((E, R, D), BF16),
            pltpu.VMEM((C, J, E, R, D), BF16),
            pltpu.VMEM((C, J, E, R, D), F32),
            pltpu.VMEM((C, J, E, R, D), BF16),
            pltpu.VMEM((C, J, E, R, D), BF16),
            pltpu.VMEM((J, E, R, D), F32),
            pltpu.VMEM((J, E, R, D), BF16),
            pltpu.VMEM((J, E, R, D), BF16),
            pltpu.VMEM((E, R, D), BF16),
            pltpu.VMEM((E, R, D), BF16),
            pltpu.VMEM((C, J, E, MT, D), BF16),
            pltpu.VMEM((NT, D), BF16),
            pltpu.VMEM((N, 1, 3 * NT), F32),
            dma((5,)),
            dma((2, K, E)),
            dma((2, K, J)),
            dma((2, K, C)),
            dma((2, K, C)),
            dma((2, K, J)),
            dma((2, K, E)),
            dma((K,)),
            dma((K,)),
            dma((K, S)),
            dma((K,)),
            dma((2, K, E)),
            dma((2, K, J)),
            dma((2, K, C)),
            dma((N,)),
            dma((N,)),
        ],
        compiler_params=pltpu.CompilerParams(
            collective_id=0, has_side_effects=True, vmem_limit_bytes=60 * 1024 * 1024
        ),
        name="relay_experts",
    )(
        hidden_in.reshape(MT, D),
        layer_gain,
        router[0].T,
        w_gate[0],
        w_up[0],
        w_down[0],
        final_gain.reshape(1, D),
        head,
        routing[0].reshape(MT, top),
        both[0:1],
        both[1:2],
    )
    return tok.reshape(M, T), seq.reshape(M, SEQS)


def solution(mesh):
    return jax.shard_map(
        body,
        mesh=mesh,
        in_specs=(
            P(None, "expert", None),
            P("section", None),
            P("section", None, None),
            P("section", None, "expert"),
            P("section", None, "expert"),
            P("section", "expert", None),
            P(),
            P(("section", "expert"), None),
            P("section", None, "expert", None),
            P(),
            P(),
        ),
        out_specs=(P(None, "expert"), P()),
        check_vma=False,
    )
```

time: 334 us -> 102 us (0.31)
  waiting for transfers between devices: 141 us -> 0 us
  Pallas kernels: 0 us -> 92.6 us
  blocking collectives: 79.3 us -> 0 us
  starting transfers between devices: 38.5 us -> 0 us
  matrix products: 28 us -> 0 us
  other arithmetic: 16 us -> 1.63 us
  between operations: 14.1 us -> 0.69 us
  local copies, waits for them, and re-layouts: 15.4 us -> 6.85 us
    pallas_call x0 -> x1, Pallas kernels: none -> 92.6 us  [body(): pl.pallas_call(functools.partial(kernel, dims), out_shape=(jax.ShapeDtype...]
    all_to_all x6 -> x0, waiting for transfers between devices: 70.8 us -> none  [the longest x3 39.2 us: expert_rows(): lax.all_to_all(partial_value.reshape(sources, slot_count, width_in), 'exp...]
    all_gather x1 -> x0, waiting for transfers between devices: 42.9 us -> none  [body(): lax.all_gather(shared, 'expert', axis=1, tiled=True)]
    psum x1 -> x0, blocking collectives: 40.9 us -> none  [body(): lax.psum((local_sum, target_part), ('section', 'expert'))]
    pmax x1 -> x0, blocking collectives: 38.4 us -> none  [body(): peak = lax.pmax(local_max, ('section', 'expert'))]
    dot_general x13 -> x0, matrix products: 28 us -> none  [the longest x3 13.8 us: expert_rows(): jnp.dot(inner, w_down[0], preferred_element_type=jnp.float32)]
    all_to_all x6 -> x0, starting transfers between devices: 26.4 us -> none  [the longest x3 15 us: expert_layer(): lax.all_to_all(outgoing, 'expert', split_axis=0, concat_axis=0, tiled=True)]
    psum x1 -> x0, waiting for transfers between devices: 21.4 us -> none  [broadcast(): return lax.psum(block, axis)]
  transfers between devices with their start and end apart: 11 -> 0, of which waited for: 11 -> 0; matrix products, arithmetic and copies ran while one was open for 3% -> 0% of each run, Pallas kernels for 0% -> 0%
where the time goes in v1:
time: 102 us
  Pallas kernels  92.6 us (91%)
  local copies, waits for them, and re-layouts  6.85 us (7%)
  other arithmetic  1.63 us (2%)
    pallas_call x1, Pallas kernels, body(): pl.pallas_call(functools.partial(kernel, dims), out_shape=(jax.ShapeDtype...  92.6 us

profile of v1, /device:TPU:0, one launch (start us, length us, event | category | flops | bytes accessed | tf_op | source)
XLA Modules:
  0.0 101.8 jit_solution(8454167847397663088)
XLA Ops:
  0.6 0.8 stack.9
  1.4 0.8 stack.10
  2.3 0.7 slice.13.tgt
  2.9 0.7 slice.15.seq
  3.6 1.3 %reshape.25.fgain = f32[1,3584]{1,0:T(1,128)} reshape(f32[3584]{0:T(1024)} %param.17) | data formatting | bytes 28672 | tf_op jit(solution)/shard_map/reshape | solution.py:476
  4.9 1.3 %copy.21 = s32[1,2,8,2]{3,2,1,0:T(8,128)} copy(s32[1,2,8,2]{2,3,1,0:T(2,128)} %param.19) | data formatting | bytes 256 | tf_op jit(solution)/shard_map/reshape;squeeze | solution.py:478
  6.3 92.6 %relay_experts.1 = (f32[16,1]{1,0:T(8,128)}, f32[8,1]{1,0:T(8,128)}) custom-call(bf16[16,3584]{1,0:T(8,128)(2,1)} %bitcast.13, f32[1,3584]{1,0:T(1,128)} %gain.1, bf16[4,3584]{1,0:T(4,128)(2,1)} %bitcast.15, bf16[3584,512]{1,0:T(8,128)(2,1)} %bitcast.10, bf16[3584,512]{1,0:T(8,128)(2,1)} %bitcast.11, bf16[512,3584]{1,0:T(8,128)(2,1)} %bitcast.12, ...), custom_call_target="tpu_custom_call" | custom-call | tf_op jit(solution)/shard_map/relay_experts/pallas_call | solution.py:420
  98.9 0.8 reduce
  99.7 0.6 reshape.26
  100.3 0.8 reduce.1
  101.1 0.6 reshape.27
  (4 shorter events, 0.0 us)

commit v2 on v1

--- a/solution.py
+++ b/solution.py
@@ -8,7 +8,8 @@
 from jax.sharding import PartitionSpec as P
 
 SEQS = 4
-CHUNKS = 2
+CHUNKS = 4
+PAIR_FIRST = 1
 F32 = jnp.float32
 BF16 = jnp.bfloat16
 
@@ -23,13 +24,12 @@
     dims,
     hid, gain, router, wg_hbm, wu_hbm, wd_hbm, fgain, head_hbm, route, tgt, seq,
     tok_out, seq_out,
-    wg, wu, wd, head, stin, stout, pack, xbuf, pf, pb, cr, qf, qb, yr, sb, ret, fin, nb, stats,
-    loc, dz, dy, dc, rc, ry, rz, xs, xr, fs, fr, az, ay, ac, ss, sr,
+    wg, wu, wd, head, stin, stout, pack, xbuf, pf, pb, cr, qf, qb, yr, sb, ret, fin, nb, stats, merged,
+    loc, dz, dy, dc, rc, ry, rz, xs, xr, fs, fr, az, ay, ac, ss, sr, ms, mr,
 ):
     S, E, J, C, R, M, T, cap, K = dims
     F = J * C
     members = E * F
-    N = S * members
     MT = M * T
     D = stin.shape[1]
     Dc = D // K
@@ -69,30 +69,49 @@
 
     barrier = pltpu.get_barrier_semaphore()
 
+    group = S * F
+    place_in = sec * F + mem % F
+
+    def group_peer(d):
+        other = (place_in + d) % group
+        return other, other // F, e * F + other % F
+
     def greet(d, carry):
-        peer = (me + d) % N
+        other, other_sec, other_mem = group_peer(d)
         pl.semaphore_signal(
-            barrier, inc=1, device_id=(peer // members, peer % members),
+            barrier, inc=1, device_id=(other_sec, other_mem),
             device_id_type=pl.DeviceIdType.MESH,
         )
         return carry
 
-    lax.fori_loop(1, N, greet, 0)
-
-    lanes = lax.broadcasted_iota(jnp.int32, (MT, E * R), 1)
-    rows = lax.broadcasted_iota(jnp.int32, (MT, E * R), 0)
-    hit = route[:, 0:1] == lanes // R
-    for k in range(1, route.shape[1]):
-        hit = hit | (route[:, k : k + 1] == lanes // R)
-    hit_f = hit.astype(F32)
+    lax.fori_loop(1, group, greet, 0)
+    for d in range(1, E):
+        pl.semaphore_signal(
+            barrier, inc=1, device_id=(sec, member((e + d) % E, j, c)),
+            device_id_type=pl.DeviceIdType.MESH,
+        )
+
+    rows = lax.broadcasted_iota(jnp.int32, (E * R, MT), 0)
+    lanes = lax.broadcasted_iota(jnp.int32, (E * R, MT), 1)
+    from_row = lax.broadcasted_iota(jnp.int32, (T, MT), 0)
+    to_lane = lax.broadcasted_iota(jnp.int32, (T, MT), 1)
+    chosen = None
+    for m in range(M):
+        lift = (to_lane == from_row + m * T).astype(BF16)
+        ids = jnp.dot(route[m].astype(F32).astype(BF16), lift, preferred_element_type=F32)
+        chosen = ids if chosen is None else chosen + ids
+    row_expert = (rows // R).astype(F32)
+    hit = chosen[0:1, :] == row_expert
+    for k in range(1, chosen.shape[0]):
+        hit = hit | (chosen[k : k + 1, :] == row_expert)
     row_a = lax.broadcasted_iota(jnp.int32, (MT, MT), 0)
     row_b = lax.broadcasted_iota(jnp.int32, (MT, MT), 1)
-    earlier = ((row_b < row_a) & (row_a // T == row_b // T)).astype(BF16)
-    rank = jnp.dot(earlier, hit_f.astype(BF16), preferred_element_type=F32)
-    place = rank + ((rows // T) * cap).astype(F32)
-    table = jnp.where(hit & (place == (lanes % R).astype(F32)), 1.0, 0.0).astype(F32)
-
-    pl.semaphore_wait(barrier, N - 1)
+    earlier = ((row_a < row_b) & (row_a // T == row_b // T)).astype(BF16)
+    rank = jnp.dot(hit.astype(BF16), earlier, preferred_element_type=F32)
+    place = rank + ((lanes // T) * cap).astype(F32)
+    table = jnp.where(hit & (place == (rows % R).astype(F32)), 1.0, 0.0).astype(F32)
+
+    pl.semaphore_wait(barrier, group - 1 + E - 1)
 
     sends = []
 
@@ -110,9 +129,8 @@
 
     table_b = table.astype(BF16)
     for k in range(K):
-        packed = lax.dot_general(
-            table_b, normed[:, k * Dc : (k + 1) * Dc], (((0,), (0,)), ((), ())),
-            preferred_element_type=F32,
+        packed = jnp.dot(
+            table_b, normed[:, k * Dc : (k + 1) * Dc], preferred_element_type=F32
         ).reshape(E, R, Dc)
         pack[:, :, cols[k]] = packed.astype(BF16)
         for d in range(1, E):
@@ -126,13 +144,14 @@
         xbuf[c, j, e, :, cols[k]] = pack[e, :, cols[k]]
 
     logits = lax.dot_general(
-        normed, router[...], (((1,), (1,)), ((), ())), preferred_element_type=F32
+        router[...], normed, (((1,), (1,)), ((), ())), preferred_element_type=F32
     )
-    spread = jnp.zeros((MT, E * R), F32)
+    spread = jnp.zeros((E * R, MT), F32)
     for i in range(E):
-        spread = jnp.where(lanes // R == i, logits[:, i : i + 1], spread)
+        spread = jnp.where(rows // R == i, logits[i : i + 1, :], spread)
     weight = jax.nn.sigmoid(spread) * table
-    weight = weight / jnp.sum(weight, -1, keepdims=True)
+    weight = weight / jnp.sum(weight, 0, keepdims=True)
+    weight = weight.T
     weight_hi = weight.astype(BF16)
     weight_lo = (weight - weight_hi.astype(F32)).astype(BF16)
 
@@ -241,6 +260,49 @@
             fs.at[k, d], fr.at[k], sec - d, mem,
         )
 
+    def column(k, b):
+        if k < PAIR_FIRST:
+            return fin.at[c, :, b, :, cols[k]]
+        return fin.at[c, j, b, :, cols[k]]
+
+    def to_experts(k, d):
+        return remote(
+            column(k, e), column(k, e), az.at[0, k, d], az.at[1, k, d],
+            sec, member((e + d) % E, j, c),
+        )
+
+    def from_experts(k, d):
+        se = (e + E - d) % E
+        return remote(
+            column(k, se), column(k, se), az.at[0, k, d], az.at[1, k, d], sec, member(se, j, c)
+        )
+
+    def pair_ref(k, pj):
+        if k < PAIR_FIRST:
+            return fin.at[c, pj, e, :, cols[k]]
+        return fin.at[c, pj, :, :, cols[k]]
+
+    def to_pair(k, d):
+        return remote(
+            pair_ref(k, j), pair_ref(k, j), ay.at[0, k, d], ay.at[1, k, d],
+            sec, member(e, (j + d) % J, c),
+        )
+
+    def from_pair(k, d):
+        sj = (j + J - d) % J
+        return remote(
+            pair_ref(k, sj), pair_ref(k, sj), ay.at[0, k, d], ay.at[1, k, d],
+            sec, member(e, sj, c),
+        )
+
+    def launch(k):
+        if k < PAIR_FIRST:
+            for d in range(1, J):
+                to_pair(k, d).start()
+        else:
+            for d in range(1, E):
+                to_experts(k, d).start()
+
     for k in range(K):
         for d in range(1, E):
             se = (e + E - d) % E
@@ -264,40 +326,30 @@
             fin[c, j, e, :, cols[k]] = result
             for d in range(1, S):
                 spread_out(k, d).start()
-
-    for k in range(K):
-        @pl.when(sec < S - 1)
-        def _():
+            launch(k)
+
+    @pl.when(sec < S - 1)
+    def _():
+        for k in range(K):
             spread_out(k, 0).wait_recv()
-
-        for d in range(1, E):
-            copy = remote(
-                fin.at[c, j, e, :, cols[k]], fin.at[c, j, e, :, cols[k]],
-                az.at[0, k, d], az.at[1, k, d], sec, member((e + d) % E, j, c),
-            )
-            copy.start()
-            sends.append(copy)
-    for k in range(K):
-        for d in range(1, E):
-            se = (e + E - d) % E
-            remote(
-                fin.at[c, j, se, :, cols[k]], fin.at[c, j, se, :, cols[k]],
-                az.at[0, k, d], az.at[1, k, d], sec, member(se, j, c),
-            ).wait_recv()
+            launch(k)
+
+    for k in range(PAIR_FIRST):
         for d in range(1, J):
-            copy = remote(
-                fin.at[c, j, :, :, cols[k]], fin.at[c, j, :, :, cols[k]],
-                ay.at[0, k, d], ay.at[1, k, d], sec, member(e, (j + d) % J, c),
-            )
-            copy.start()
-            sends.append(copy)
-    for k in range(K):
-        for d in range(1, J):
-            sj = (j + J - d) % J
-            remote(
-                fin.at[c, sj, :, :, cols[k]], fin.at[c, sj, :, :, cols[k]],
-                ay.at[0, k, d], ay.at[1, k, d], sec, member(e, sj, c),
-            ).wait_recv()
+            from_pair(k, d).wait_recv()
+        for d in range(1, E):
+            to_experts(k, d).start()
+    late = list(range(PAIR_FIRST, K)) + list(range(PAIR_FIRST))
+    for k in late:
+        for d in range(1, E):
+            from_experts(k, d).wait_recv()
+        if k >= PAIR_FIRST:
+            for d in range(1, J):
+                to_pair(k, d).start()
+    for k in late[::-1]:
+        if k >= PAIR_FIRST:
+            for d in range(1, J):
+                from_pair(k, d).wait_recv()
         for d in range(1, C):
             copy = remote(
                 fin.at[c, :, :, :, cols[k]], fin.at[c, :, :, :, cols[k]],
@@ -313,34 +365,45 @@
                 ac.at[0, k, d], ac.at[1, k, d], sec, member(e, j, sc),
             ).wait_recv()
 
-    for pc in range(C):
-        for pj in range(J):
-            block = fin[pc, pj].reshape(E * MT, D)
-            base = (pc * J + pj) * E * MT
-            nb[base : base + E * MT, :] = rms_scale(block, fgain[...]).astype(BF16)
+    for pj in range(J):
+        for pe in range(E):
+            blocks = [
+                rms_scale(fin[pc, pj, pe], fgain[...].reshape(1, D)) for pc in range(C)
+            ]
+            for m in range(M):
+                base = m * members * T + member(pe, pj, 0) * T
+                piece = jnp.concatenate([b[m * T : (m + 1) * T, :] for b in blocks], 0)
+                nb[base : base + C * T, :] = piece.astype(BF16)
     locals_[3].wait()
     scores = lax.dot_general(
         head[...], nb[...], (((1,), (1,)), ((), ())), preferred_element_type=F32
     )
     vocab = me * voc + lax.broadcasted_iota(jnp.int32, (voc, NT), 0)
-    own_target = jnp.sum(jnp.where(vocab == tgt[...], scores, 0.0), 0, keepdims=True)
+    aims = jnp.concatenate([tgt[m : m + 1, :] for m in range(M)], 1)
+    own_target = jnp.sum(jnp.where(vocab == aims, scores, 0.0), 0, keepdims=True)
     own_max = jnp.max(scores, 0, keepdims=True)
     own_sum = jnp.sum(jnp.exp(scores - own_max), 0, keepdims=True)
-    stats[me, :, 0:NT] = own_max
-    stats[me, :, NT : 2 * NT] = own_sum
-    stats[me, :, 2 * NT : 3 * NT] = own_target
+    def put(ref, at, values):
+        for i, value in enumerate(values):
+            ref[at, :, i * NT : (i + 1) * NT] = value
+
+    def merge(ref):
+        maxes = ref[:, :, 0:NT]
+        top = jnp.max(maxes, 0)
+        total = jnp.sum(jnp.exp(maxes - top[None]) * ref[:, :, NT : 2 * NT], 0)
+        return top, total, jnp.sum(ref[:, :, 2 * NT : 3 * NT], 0)
+
+    put(stats, place_in, (own_max, own_sum, own_target))
 
     def tell(d):
-        peer = (me + d) % N
+        other, other_sec, other_mem = group_peer(d)
         return remote(
-            stats.at[me], stats.at[me], ss.at[d], sr.at[d], peer // members, peer % members
+            stats.at[place_in], stats.at[place_in], ss.at[d], sr.at[d], other_sec, other_mem
         )
 
     def hear(d):
-        peer = (me + N - d) % N
-        return remote(
-            stats.at[peer], stats.at[peer], ss.at[d], sr.at[d], peer // members, peer % members
-        )
+        other, other_sec, other_mem = group_peer(group - d)
+        return remote(stats.at[other], stats.at[other], ss.at[d], sr.at[d], other_sec, other_mem)
 
     def tell_all(d, carry):
         tell(d).start()
@@ -350,24 +413,40 @@
         hear(d).wait_recv()
         return carry
 
-    lax.fori_loop(1, N, tell_all, 0)
-    lax.fori_loop(1, N, hear_all, 0)
-    maxes = stats[:, :, 0:NT]
-    peak = jnp.max(maxes, 0)
-    total = jnp.sum(jnp.exp(maxes - peak[None]) * stats[:, :, NT : 2 * NT], 0)
-    target_logit = jnp.sum(stats[:, :, 2 * NT : 3 * NT], 0)
+    lax.fori_loop(1, group, tell_all, 0)
+    lax.fori_loop(1, group, hear_all, 0)
+    put(merged, e, merge(stats))
+    for d in range(1, E):
+        copy = remote(
+            merged.at[e], merged.at[e], ms.at[d], mr.at[d], sec, member((e + d) % E, j, c)
+        )
+        copy.start()
+        sends.append(copy)
+    for d in range(1, E):
+        se = (e + E - d) % E
+        remote(
+            merged.at[se], merged.at[se], ms.at[d], mr.at[d], sec, member(se, j, c)
+        ).wait_recv()
+    peak, total, target_logit = merge(merged)
     logprob = target_logit - (peak + jnp.log(total))
 
-    own = ((c * J + j) * E + e) * MT
-    lane = lax.broadcasted_iota(jnp.int32, (MT, NT), 1)
-    row = lax.broadcasted_iota(jnp.int32, (MT, NT), 0)
-    tok_out[...] = jnp.sum(jnp.where(lane == own + row, logprob, 0.0), -1, keepdims=True)
-    lane = lax.broadcasted_iota(jnp.int32, (M * SEQS, NT), 1)
-    row = lax.broadcasted_iota(jnp.int32, (M * SEQS, NT), 0)
-    inside = ((lane % MT) // T == row // SEQS) & (seq[...] == row % SEQS)
-    sums = jnp.sum(jnp.where(inside, logprob, 0.0), -1, keepdims=True)
-    counts = jnp.sum(jnp.where(inside, 1.0, 0.0), -1, keepdims=True)
-    seq_out[...] = sums / counts
+    def across(column, count):
+        a = lax.broadcasted_iota(jnp.int32, (count, count), 0)
+        b = lax.broadcasted_iota(jnp.int32, (count, count), 1)
+        return jnp.sum(jnp.where(a == b, column, 0.0), 0, keepdims=True)
+
+    tokens = members * T
+    lane = lax.broadcasted_iota(jnp.int32, (T, tokens), 1)
+    row = lax.broadcasted_iota(jnp.int32, (T, tokens), 0)
+    row_s = lax.broadcasted_iota(jnp.int32, (SEQS, tokens), 0)
+    for m in range(M):
+        line = logprob[:, m * tokens : (m + 1) * tokens]
+        own = jnp.sum(jnp.where(lane == mem * T + row, line, 0.0), -1, keepdims=True)
+        tok_out[m : m + 1, :] = across(own, T)
+        inside = seq[m : m + 1, :] == row_s
+        sums = jnp.sum(jnp.where(inside, line, 0.0), -1, keepdims=True)
+        counts = jnp.sum(jnp.where(inside, 1.0, 0.0), -1, keepdims=True)
+        seq_out[m : m + 1, :] = across(sums / counts, SEQS)
 
     for copy in sends:
         copy.wait_send()
@@ -387,7 +466,12 @@
         tell(d).wait_send()
         return carry
 
-    lax.fori_loop(1, N, told_all, 0)
+    lax.fori_loop(1, group, told_all, 0)
+    for k in range(K):
+        for d in range(1, E):
+            to_experts(k, d).wait_send()
+        for d in range(1, J):
+            to_pair(k, d).wait_send()
 
 
 def body(
@@ -408,11 +492,7 @@
     NT = members * MT
     ff = w_gate.shape[2]
     voc = head.shape[0]
-    N = S * members
     dims = (S, E, J, C, R, M, T, cap, K)
-
-    both = jnp.stack([targets, seq_ids]).reshape(2, M, E, J, C, T)
-    both = both.transpose(0, 4, 3, 2, 1, 5).reshape(2, NT)
 
     vmem = pl.BlockSpec(memory_space=pltpu.VMEM)
     hbm = pl.BlockSpec(memory_space=pl.ANY)
@@ -420,8 +500,8 @@
     tok, seq = pl.pallas_call(
         functools.partial(kernel, dims),
         out_shape=(
-            jax.ShapeDtypeStruct((MT, 1), F32),
-            jax.ShapeDtypeStruct((M * SEQS, 1), F32),
+            jax.ShapeDtypeStruct((M, T), F32),
+            jax.ShapeDtypeStruct((M, SEQS), F32),
         ),
         in_specs=[hbm, vmem, vmem, hbm, hbm, hbm, vmem, hbm, vmem, vmem, vmem],
         out_specs=(vmem, vmem),
@@ -444,7 +524,8 @@
             pltpu.VMEM((E, R, D), BF16),
             pltpu.VMEM((C, J, E, MT, D), BF16),
             pltpu.VMEM((NT, D), BF16),
-            pltpu.VMEM((N, 1, 3 * NT), F32),
+            pltpu.VMEM((S * F, 1, 3 * NT), F32),
+            pltpu.VMEM((E, 1, 3 * NT), F32),
             dma((5,)),
             dma((2, K, E)),
             dma((2, K, J)),
@@ -459,8 +540,10 @@
             dma((2, K, E)),
             dma((2, K, J)),
             dma((2, K, C)),
-            dma((N,)),
-            dma((N,)),
+            dma((S * F,)),
+            dma((S * F,)),
+            dma((E,)),
+            dma((E,)),
         ],
         compiler_params=pltpu.CompilerParams(
             collective_id=0, has_side_effects=True, vmem_limit_bytes=60 * 1024 * 1024
@@ -473,13 +556,13 @@
         w_gate[0],
         w_up[0],
         w_down[0],
-        final_gain.reshape(1, D),
+        final_gain,
         head,
-        routing[0].reshape(MT, top),
-        both[0:1],
-        both[1:2],
+        routing[0].transpose(0, 2, 1),
+        targets,
+        seq_ids,
     )
-    return tok.reshape(M, T), seq.reshape(M, SEQS)
+    return tok, seq
 
 
 def solution(mesh):

time: 102 us -> 88 us (0.86)
  Pallas kernels: 92.6 us -> 84.7 us
  local copies, waits for them, and re-layouts: 6.85 us -> 2.44 us
  other arithmetic: 1.63 us -> 0 us
    pallas_call x1, Pallas kernels: 92.6 us -> 84.7 us  [body(): pl.pallas_call(functools.partial(kernel, dims), out_shape=(jax.ShapeDtype...]
    another operation x5 -> x0, local copies, waits for them, and re-layouts: 2.91 us -> none  [the longest x4 1.57 us: body(): both = jnp.stack([targets, seq_ids]).reshape(2, M, E, J, C, T)]
    reshape x3 -> x0, local copies, waits for them, and re-layouts: 2.61 us -> none  [the longest x1 1.32 us: body(): final_gain.reshape(1, D)]
    unnamed x0 -> x2, local copies, waits for them, and re-layouts: none -> 2.44 us
    pallas_call x2 -> x0, other arithmetic: 1.61 us -> none  [body(): pl.pallas_call(functools.partial(kernel, dims), out_shape=(jax.ShapeDtype...]
    slice x3 -> x0, local copies, waits for them, and re-layouts: 1.32 us -> none  [the longest x2 0.66 us: body(): both[1:2]]
where the time goes in v2:
time: 88 us; the launch traced here: 87.8 us
  Pallas kernels  84.7 us (96%)
  local copies, waits for them, and re-layouts  2.44 us (3%)
    pallas_call x1, Pallas kernels, body(): pl.pallas_call(functools.partial(kernel, dims), out_shape=(jax.ShapeDtype...  84.7 us
    unnamed x2, local copies, waits for them, and re-layouts  2.44 us

profile of v2, /device:TPU:0, one launch (start us, length us, event | category | flops | bytes accessed | tf_op | source)
XLA Modules:
  0.0 87.8 jit_solution(9216987559332267205)
XLA Ops:
  0.6 84.7 %relay_experts.1 = (f32[2,8]{1,0:T(2,128)}, f32[2,4]{1,0:T(2,128)}) custom-call(bf16[16,3584]{1,0:T(8,128)(2,1)} %bitcast.13, f32[1,3584]{1,0:T(1,128)} %gain.1, bf16[4,3584]{1,0:T(4,128)(2,1)} %bitcast.14, bf16[3584,512]{1,0:T(8,128)(2,1)} %bitcast.10, bf16[3584,512]{1,0:T(8,128)(2,1)} %bitcast.11, bf16[512,3584]{1,0:T(8,128)(2,1)} %bitcast.12, ...), custom_call_target="tpu_custom_call" | custom-call | tf_op jit(solution)/shard_map/relay_experts/pallas_call | solution.py:500
  85.4 1.2 %copy.15 = f32[2,8]{1,0:T(2,128)} copy(f32[2,8]{1,0:T(2,128)} %get-tuple-element.4) | data formatting | bytes 128
  86.6 1.2 %copy.16 = f32[2,4]{1,0:T(2,128)} copy(f32[2,4]{1,0:T(2,128)} %get-tuple-element.5) | data formatting | bytes 64
